TPU v7x, 32 devices: a whole 2x2x4 slice. The times are simulated.
32 devices in a mesh: pipe: 2 (over core), dp: 8 (over z, y), mp: 2 (over x).
Axes of the slice: x: 2, y: 2, z: 4, core: 2. Of those that a mesh axis runs over, the one named last changes fastest.
Arguments:
- token_ids: int32 [2, 4096], P('pipe', 'dp'), may hold values from 0 to 32127, as said below
- embedded: bfloat16 [2, 4096, 4096], P('pipe', 'dp', 'mp'), may hold values from -720 to 720
- norm_gain: float32 [2, 4096], P('pipe', 'mp'), may hold values from 0.25 to 1.75
- proj_grad: bfloat16 [2, 4096, 2048], P('pipe', 'dp'), may hold values from -6 to 6
- proj_weight: bfloat16 [2, 4096, 2048], P('pipe', 'mp'), may hold values from -0.125 to 0.125
- stream_grad: bfloat16 [2, 4096, 4096], P('pipe', 'dp', 'mp'), may hold values from -6 to 6
Outputs:
- table_grad: float32 [32128, 2, 2048], P('dp', 'mp', 'pipe')
Inputs may be any that keep to these rules, and one draw needn't show every extreme that they name: `token_ids`: call block o the ids o * 4016 to (o + 1) * 4016 - 1. The 512 tokens of one stack on one index of dp hold at most 128 ids of any one block, and some block gets exactly 128 of them.
All inputs are finite; a program needn't handle non-finite values.
Results may differ from a plain program's by a relative error of at most 0.0029.
Values may be sent and summed in bfloat16 or wider, within the bound.
A program may use at most 128 MiB of HBM per device.

v0:
```python
import jax
import jax.numpy as jnp
from jax import lax
from jax.sharding import PartitionSpec as P

D = 4096
VOCAB = 32128


epsilon = 1e-06


def accumulate(got_rows, got_index, block_rows):
    width = got_rows.shape[-1]
    flat_rows = got_rows.reshape(-1, width)
    flat_index = got_index.reshape(-1)
    selector = (flat_index[None, :] == jnp.arange(block_rows, dtype=jnp.int32)[:, None]).astype(
        jnp.bfloat16
    )
    return jnp.dot(selector, flat_rows, preferred_element_type=jnp.float32)


def on_device(token_ids, embedded, norm_gain, proj_grad, proj_weight, stream_grad):
    projected = lax.dot_general(
        proj_grad[0], proj_weight[0], (((1,), (1,)), ((), ())), preferred_element_type=jnp.float32
    )
    inputs = embedded[0].astype(jnp.float32)
    scaled = projected * norm_gain[0][None, :]
    square_sum, mixed_sum = lax.psum(
        (jnp.sum(inputs * inputs, axis=1), jnp.sum(inputs * scaled, axis=1)), "mp"
    )
    inverse = lax.rsqrt(square_sum / D + epsilon)
    norm_back = (
        inverse[:, None] * scaled - inputs * (inverse * inverse * inverse * mixed_sum / D)[:, None]
    )
    grad_rows = (stream_grad[0].astype(jnp.float32) + norm_back).astype(jnp.bfloat16)
    replicas = lax.axis_size("dp")
    tokens_here = grad_rows.shape[0]
    capacity = max(2, 2 * tokens_here // replicas)
    block_rows = VOCAB // replicas
    token_row = token_ids[0]
    owners = token_row // block_rows
    local_row = token_row % block_rows
    matches = (owners[:, None] == jnp.arange(replicas, dtype=jnp.int32)[None, :]).astype(jnp.int32)
    earlier = jnp.cumsum(matches, axis=0) - matches
    position = owners * capacity + jnp.sum(earlier * matches, axis=1)
    placer = (
        position[None, :] == jnp.arange(replicas * capacity, dtype=jnp.int32)[:, None]
    ).astype(jnp.bfloat16)
    send_rows = jnp.dot(placer, grad_rows, preferred_element_type=jnp.float32).astype(jnp.bfloat16)
    send_rows = send_rows.reshape(replicas, capacity, grad_rows.shape[1])
    send_index = jnp.full((replicas * capacity,), block_rows, jnp.int32).at[position].set(local_row)
    send_index = send_index.reshape(replicas, capacity)
    paired_index = jnp.stack([send_index, send_index], axis=2)
    mixed_rows, mixed_index = (
        lax.all_to_all(send_rows, "pipe", split_axis=2, concat_axis=1, tiled=True),
        lax.all_to_all(paired_index, "pipe", split_axis=2, concat_axis=1, tiled=True),
    )
    got_rows, got_index = (
        lax.all_to_all(mixed_rows, "dp", split_axis=0, concat_axis=0, tiled=True),
        lax.all_to_all(mixed_index, "dp", split_axis=0, concat_axis=0, tiled=True),
    )
    half_table = accumulate(got_rows, got_index, block_rows)
    return half_table.reshape(block_rows, 1, half_table.shape[1])


def solution(mesh):
    return jax.shard_map(
        on_device,
        mesh=mesh,
        in_specs=(
            P("pipe", "dp"),
            P("pipe", "dp", "mp"),
            P("pipe", "mp"),
            P("pipe", "dp", None),
            P("pipe", "mp", None),
            P("pipe", "dp", "mp"),
        ),
        out_specs=P("dp", "mp", "pipe"),
        check_vma=False,
    )
```

profile of v0, /device:TPU:0, one launch (start us, length us, event | category | flops | bytes accessed | tf_op | source)
XLA Modules:
  0.0 245.0 jit_solution(3031371806581677621)
XLA Ops:
  0.0 0.0 copy-start
  0.0 0.9 compare_reduce_fusion
  0.9 0.7 broadcast_remainder_fusion
  1.6 1.1 reduce-window.6
  2.7 0.2 slice_reduce_fusion
  3.0 0.1 fusion.19
  3.1 0.7 compare_select_fusion
  3.8 2.4 scatter_custom_fusion
  6.3 0.6 pad_add_fusion
  6.8 3.2 %all-to-all-start = ((s32[8,128,2]{1,0,2:T(8,128)}), s32[8,128,2]{1,0,2:T(8,128)S(1)}, u32[]{:S(2)}, u32[]{:S(2)}) async-start(s32[8,128,2]{1,0,2:T(8,128)} %pad_add_fusion), calls=%async_computation | async-start | bytes 16384 | tf_op jit(solution)/shard_map/all_to_all | solution.py:57
  10.1 0.7 fusion.22
  10.8 0.0 copy-done
  10.8 0.0 copy-start.2
  10.8 10.0 %fusion.5 = (f32[512]{0:T(512)S(1)}, f32[512]{0:T(512)S(1)}, f32[512,2048]{1,0:T(8,128)}) fusion(bf16[1,512,2048]{2,1,0:T(8,128)(2,1)} %param.7, f32[2048]{0:T(1024)} %bitcast.84, bf16[1,2048,2048]{2,1,0:T(8,128)(2,1)} %param.10, bf16[1,512,2048]{2,1,0:T(8,128)(2,1)S(1)} %copy-done), kind=kOutput, calls=%fused_computation.10 | convolution fusion | flops 4301257728 | bytes 16789504 | tf_op jit(solution)/shard_map/dot_general | solution.py:24
  20.8 5.8 %all-reduce = (f32[512]{0:T(512)S(1)}, f32[512]{0:T(512)S(1)}) all-reduce(f32[512]{0:T(512)S(1)} %get-tuple-element.6, f32[512]{0:T(512)S(1)} %get-tuple-element.5), channel_id=1, replica_groups=mesh['pipe'=2,'dp'=8,'mp'=2] {'mp'}, use_global_device_ids=true, to_apply=%region_7.8 | all-reduce | flops 1024 | bytes 8192 | tf_op jit(solution)/shard_map/psum | solution.py:29
  26.7 0.0 copy-done.2
  26.7 8.1 %convolution_convert_fusion = bf16[1024,2048]{1,0:T(8,128)(2,1)} fusion(f32[512,2048]{1,0:T(8,128)} %get-tuple-element.17, bf16[1,512,2048]{2,1,0:T(8,128)(2,1)} %param.11, bf16[1,512,2048]{2,1,0:T(8,128)(2,1)} %param.7, f32[512]{0:T(512)S(1)} %get-tuple-element.16, f32[2048]{0:T(1024)S(1)} %bitcast.85, f32[512]{0:T(512)S(1)} %get-tuple-element.15, ...), kind=kOutput, calls=%fused_computation.15 | convolution fusion | flops 2158493696 | bytes 12597248 | tf_op jit(solution)/shard_map/dot_general | solution.py:50
  34.8 6.8 %copy.13 = bf16[8,128,2048]{1,0,2:T(8,128)(2,1)} copy(bf16[8,128,2048]{2,1,0:T(8,128)(2,1)} %bitcast.72) | data formatting | bytes 8388608 | tf_op jit(solution)/shard_map/reshape | solution.py:51
  41.6 0.0 all-to-all-done
  41.6 5.6 %all-to-all-start.2 = ((bf16[8,128,2048]{1,0,2:T(8,128)(2,1)}), bf16[8,128,2048]{1,0,2:T(8,128)(2,1)}, u32[]{:S(2)}, u32[]{:S(2)}) async-start(bf16[8,128,2048]{1,0,2:T(8,128)(2,1)} %copy.13), calls=%async_computation.2 | async-start | bytes 8388608 | tf_op jit(solution)/shard_map/all_to_all | solution.py:56
  47.2 0.6 copy.12
  47.8 3.9 %all-to-all-done.2 = bf16[8,128,2048]{1,0,2:T(8,128)(2,1)} async-done(((bf16[8,128,2048]{1,0,2:T(8,128)(2,1)}), bf16[8,128,2048]{1,0,2:T(8,128)(2,1)}, u32[]{:S(2)}, u32[]{:S(2)}) %all-to-all-start.2) | async-done | bytes 4194336 | tf_op jit(solution)/shard_map/all_to_all | solution.py:56
  51.7 6.4 %all-to-all-start.1 = ((s32[8,256,1]{1,2,0:T(1,128)}), s32[8,256,1]{1,2,0:T(1,128)S(1)}, u32[]{:S(2)}, u32[]{:S(2)}) async-start(s32[8,256,1]{1,2,0:T(1,128)} %copy.12), calls=%async_computation.1 | async-start | bytes 16384 | tf_op jit(solution)/shard_map/all_to_all | solution.py:61
  58.0 6.6 %copy.15 = bf16[8,2,128,1024]{3,2,1,0:T(8,128)(2,1)} copy(bf16[8,2,128,1024]{2,0,3,1:T(8,128)(2,1)} %bitcast.25) | data formatting | bytes 8388608 | tf_op jit(solution)/shard_map/all_to_all | solution.py:56
  64.6 0.0 all-to-all-done.1
  64.6 99.1 %all_to_all.46 = bf16[8,256,1024]{2,1,0:T(8,128)(2,1)S(1)} all-to-all(bf16[8,256,1024]{2,1,0:T(8,128)(2,1)} %bitcast.71), channel_id=1, replica_groups=mesh['pipe'=2,'dp'=8,'mp'=2] {'dp'}, dimensions={0} | all-to-all | bytes 8388608 | tf_op jit(solution)/shard_map/all_to_all | solution.py:60
  163.8 17.4 %fusion.2 = f32[4016,1,1024]{2,0,1:T(8,128)S(1)} fusion(bf16[2048,1024]{1,0:T(8,128)(2,1)S(1)} %bitcast.73, s32[2048]{0:T(1024)S(1)} %bitcast.81), kind=kOutput, calls=%fused_computation.4 | convolution fusion | flops 16852549632 | bytes 20652032 | tf_op jit(solution)/shard_map/dot_general | solution.py:20
  181.1 0.0 copy-start.1
  181.2 63.9 %copy.16 = f32[4016,1,1024]{2,1,0:T(1,128)} copy(f32[4016,1,1024]{2,0,1:T(8,128)S(1)} %fusion.2) | data formatting | bytes 32899072 | tf_op jit(solution)/shard_map/reshape | solution.py:64
  245.0 0.0 copy-done.1
  (6 shorter events, 0.1 us)
Async XLA Ops:
  0.0 10.8 %copy-start = (bf16[1,512,2048]{2,1,0:T(8,128)(2,1)S(1)}, bf16[1,512,2048]{2,1,0:T(8,128)(2,1)}, u32[]{:S(2)}) copy-start(bf16[1,512,2048]{2,1,0:T(8,128)(2,1)} %param.9) | copy-start | bytes 6291460
  6.8 34.7 %all-to-all-start = ((s32[8,128,2]{1,0,2:T(8,128)}), s32[8,128,2]{1,0,2:T(8,128)S(1)}, u32[]{:S(2)}, u32[]{:S(2)}) async-start(s32[8,128,2]{1,0,2:T(8,128)} %pad_add_fusion), calls=%async_computation | async-start | bytes 16384 | tf_op jit(solution)/shard_map/all_to_all | solution.py:57
  10.8 15.9 %copy-start.2 = (f32[1,2048]{1,0:T(1,128)S(1)}, f32[1,2048]{1,0:T(1,128)}, u32[]{:S(2)}) copy-start(f32[1,2048]{1,0:T(1,128)} %param.8) | copy-start | bytes 24580
  41.6 10.1 %all-to-all-start.2 = ((bf16[8,128,2048]{1,0,2:T(8,128)(2,1)}), bf16[8,128,2048]{1,0,2:T(8,128)(2,1)}, u32[]{:S(2)}, u32[]{:S(2)}) async-start(bf16[8,128,2048]{1,0,2:T(8,128)(2,1)} %copy.13), calls=%async_computation.2 | async-start | bytes 8388608 | tf_op jit(solution)/shard_map/all_to_all | solution.py:56
  51.7 13.0 %all-to-all-start.1 = ((s32[8,256,1]{1,2,0:T(1,128)}), s32[8,256,1]{1,2,0:T(1,128)S(1)}, u32[]{:S(2)}, u32[]{:S(2)}) async-start(s32[8,256,1]{1,2,0:T(1,128)} %copy.12), calls=%async_computation.1 | async-start | bytes 16384 | tf_op jit(solution)/shard_map/all_to_all | solution.py:61
  181.1 63.9 %copy-start.1 = (bf16[1,512,2048]{2,1,0:T(8,128)(2,1)S(1)}, bf16[1,512,2048]{2,1,0:T(8,128)(2,1)}, u32[]{:S(2)}) copy-start(bf16[1,512,2048]{2,1,0:T(8,128)(2,1)} %param.9) | copy-start | bytes 6291460
where the time goes:
time: 246 us; the launch traced here: 245 us
  blocking collectives  105 us (43%)
  local copies, waits for them, and re-layouts  80.5 us (33%)
  matrix products  35.5 us (14%)
  starting transfers between devices  15.2 us (6%)
  other arithmetic  4.86 us (2%)
  waiting for transfers between devices  3.88 us (2%)
    all_to_all x1, blocking collectives, on_device(): lax.all_to_all(mixed_rows, 'dp', split_axis=0, concat_axis=0, tiled=True)  99.1 us
    reshape x1, local copies, waits for them, and re-layouts, on_device(): return half_table.reshape(block_rows, 1, half_table.shape[1])  63.9 us
    dot_general x1, matrix products, accumulate(): return jnp.dot(selector, flat_rows, preferred_element_type=jnp.float32)  17.4 us
    dot_general x1, matrix products, on_device(): lax.dot_general(proj_grad[0], proj_weight[0], (((1,), (1,)), ((), ())), p...  10 us
    dot_general x1, matrix products, on_device(): jnp.dot(placer, grad_rows, preferred_element_type=jnp.float32)  8.1 us
    reshape x1, local copies, waits for them, and re-layouts, on_device(): send_rows = send_rows.reshape(replicas, capacity, grad_rows.shape[1])  6.76 us
    all_to_all x1, local copies, waits for them, and re-layouts, on_device(): lax.all_to_all(send_rows, 'pipe', split_axis=2, concat_axis=1, tiled=True)  6.6 us
    all_to_all x1, starting transfers between devices, on_device(): lax.all_to_all(mixed_index, 'dp', split_axis=0, concat_axis=0, tiled=True)  6.37 us
  transfers between devices with their start and end apart: 3, of which 1 were waited for; matrix products, arithmetic and copies ran while one was open for 13% of the time, Pallas kernels for 0%

commit v1 on v0

v1 whole, which is shorter than its diff:
```python
import functools

import jax
import jax.numpy as jnp
from jax import lax
from jax.experimental import pallas as pl
from jax.experimental.pallas import tpu as pltpu
from jax.sharding import PartitionSpec as P

VOCAB = 32128
LANES = 128
epsilon = 1e-06
VMEM_LIMIT = 60 * 1024 * 1024


def partner(me, k, n):
    out, bit = 0, 1
    while bit < n:
        mine = (me // bit) % 2
        flip = (k // bit) % 2
        out = out + bit * (mine + flip - 2 * mine * flip)
        bit *= 2
    return out


def contract_last(a, b):
    return lax.dot_general(a, b, (((1,), (1,)), ((), ())), preferred_element_type=jnp.float32)


def exchange_kernel(
    n, n_mp, cap, block_rows, full_width, chunk, token_chunk,
    ids_ref, gain_ref, embedded, proj_grad, weight, stream,
    rows_out, index_out,
    emb_v, grad_v, weight_v, stream_v, scaled_v, rows_v, send_v, sendi_v, sums_v, sums_got, position_v, local_v,
    in_sem, weight_sem, sum_send, sum_recv, send_sem, recv_sem, isend_sem, irecv_sem, own_sem,
):
    pipe = lax.axis_index("pipe")
    me = lax.axis_index("dp")
    mp = lax.axis_index("mp")
    other = 1 - pipe
    tokens, width = emb_v.shape
    half = width // 2

    loads = [
        pltpu.make_async_copy(proj_grad, grad_v, in_sem.at[0]),
        pltpu.make_async_copy(embedded, emb_v, in_sem.at[1]),
        pltpu.make_async_copy(stream, stream_v, in_sem.at[2]),
    ]
    chunks = [
        pltpu.make_async_copy(
            weight.at[pl.ds(j * chunk, chunk)], weight_v.at[pl.ds(j * chunk, chunk)], weight_sem.at[j]
        )
        for j in range(width // chunk)
    ]
    loads[0].start()
    chunks[0].start()
    loads[1].start()
    for copy in chunks[1:]:
        copy.start()
    loads[2].start()

    barrier = pltpu.get_barrier_semaphore()

    def greet(k, carry):
        d = partner(me, k, n)
        pl.semaphore_signal(
            barrier, inc=1, device_id={"dp": d, "pipe": other}, device_id_type=pl.DeviceIdType.MESH
        )

        @pl.when(k > 0)
        def _():
            pl.semaphore_signal(
                barrier, inc=1, device_id={"dp": d, "pipe": pipe}, device_id_type=pl.DeviceIdType.MESH
            )

        return carry

    lax.fori_loop(0, n, greet, 0)
    pl.semaphore_signal(
        barrier, inc=1, device_id={"mp": 1 - mp}, device_id_type=pl.DeviceIdType.MESH
    )

    ids = ids_ref[...]
    owner_low = lax.broadcasted_iota(jnp.int32, (n, tokens), 0) * block_rows
    match = (ids >= owner_low) & (ids < owner_low + block_rows)
    match_f = match.astype(jnp.float32)
    before = (
        lax.broadcasted_iota(jnp.int32, (tokens, tokens), 0)
        < lax.broadcasted_iota(jnp.int32, (tokens, tokens), 1)
    ).astype(jnp.float32).astype(jnp.bfloat16)
    rank = jnp.dot(match_f.astype(jnp.bfloat16), before, preferred_element_type=jnp.float32)
    slot_low = (lax.broadcasted_iota(jnp.int32, (n, tokens), 0) * cap).astype(jnp.float32)
    position_v[...] = jnp.sum(match_f * (slot_low + rank), axis=0, keepdims=True).astype(jnp.int32)
    local = ids - jnp.sum(jnp.where(match, owner_low, 0), axis=0, keepdims=True)
    high = local // 64
    row = lax.broadcasted_iota(jnp.int32, (8, tokens), 0)
    local_v[...] = (
        jnp.where(row == 0, high, jnp.where(row == 1, local - high * 64, 0))
        .astype(jnp.float32).astype(jnp.bfloat16)
    )

    loads[0].wait()
    mixed = jnp.zeros((tokens, 1), jnp.float32)
    square = jnp.zeros((tokens, 1), jnp.float32)
    for j in range(width // chunk):
        cols = pl.ds(j * chunk, chunk)
        chunks[j].wait()
        if j == 0:
            loads[1].wait()
        scaled = contract_last(grad_v[...], weight_v[cols, :]) * gain_ref[:, cols]
        scaled_v[:, cols] = scaled
        inputs = emb_v[:, cols].astype(jnp.float32)
        square = square + jnp.sum(inputs * inputs, axis=1, keepdims=True)
        mixed = mixed + jnp.sum(inputs * scaled, axis=1, keepdims=True)
    lane = lax.broadcasted_iota(jnp.int32, (tokens, LANES), 1)
    packed = jnp.where(lane == 0, square, jnp.where(lane == 1, mixed, 0.0))
    sums_v[...] = packed.T[:8]

    pl.semaphore_wait(barrier, 2 * n)
    swap = pltpu.make_async_remote_copy(
        src_ref=sums_v, dst_ref=sums_got, send_sem=sum_send, recv_sem=sum_recv,
        device_id={"mp": 1 - mp}, device_id_type=pl.DeviceIdType.MESH,
    )
    swap.start()

    def place_index(k, carry):
        d = partner(me, k, n)
        slots = d * cap + lax.broadcasted_iota(jnp.int32, (cap, tokens), 0)
        placer = (position_v[...] == slots).astype(jnp.float32).astype(jnp.bfloat16)
        parts = contract_last(local_v[...], placer)
        sendi_v[k] = (parts[0:1] * 64.0 + parts[1:2]).astype(jnp.int32)
        return carry

    lax.fori_loop(0, n, place_index, 0)
    loads[2].wait()
    swap.wait()

    total = sums_v[...] + sums_got[...]
    inverse = lax.rsqrt(total[0:1] / full_width + epsilon)
    coef = inverse * inverse * inverse * total[1:2] / full_width
    row8 = lax.broadcasted_iota(jnp.int32, (LANES, tokens), 0)
    back = jnp.where(row8 == 0, inverse, jnp.where(row8 == 1, coef, 0.0)).T
    sums_col_inv = back[:, 0:1]
    sums_col_coef = back[:, 1:2]
    for j in range(width // chunk):
        cols = pl.ds(j * chunk, chunk)
        norm_back = sums_col_inv * scaled_v[:, cols] - emb_v[:, cols].astype(jnp.float32) * sums_col_coef
        rows_v[:, cols] = (stream_v[:, cols].astype(jnp.float32) + norm_back).astype(jnp.bfloat16)

    def row_copy(k, p, d):
        return pltpu.make_async_remote_copy(
            src_ref=send_v.at[k, p], dst_ref=rows_out.at[k, pipe],
            send_sem=send_sem.at[k, p], recv_sem=recv_sem.at[k, pipe],
            device_id={"dp": d, "pipe": p}, device_id_type=pl.DeviceIdType.MESH,
        )

    def index_copy(k, p, d):
        return pltpu.make_async_remote_copy(
            src_ref=sendi_v.at[k], dst_ref=index_out.at[k, pipe],
            send_sem=isend_sem.at[k, p], recv_sem=irecv_sem.at[k, pipe],
            device_id={"dp": d, "pipe": p}, device_id_type=pl.DeviceIdType.MESH,
        )

    def send(k):
        d = partner(me, k, n)
        row_copy(k, other, d).start()
        index_copy(k, other, d).start()

        @pl.when(k > 0)
        def _():
            row_copy(k, pipe, d).start()
            index_copy(k, pipe, d).start()

    def place(k, carry):
        k = (k + 1) % n
        d = partner(me, k, n)
        slots = d * cap + lax.broadcasted_iota(jnp.int32, (cap, tokens), 0)
        placer = (position_v[...] == slots).astype(jnp.float32).astype(jnp.bfloat16)
        for p in range(2):
            send_v[k, p] = jnp.dot(
                placer, rows_v[:, p * half:(p + 1) * half], preferred_element_type=jnp.float32
            ).astype(jnp.bfloat16)

        @pl.when(k != 1 % n)
        def _():
            send((k + n - 1) % n)

        return carry

    lax.fori_loop(0, n, place, 0)
    send(0)
    own_rows = pltpu.make_async_copy(send_v.at[0, pipe], rows_out.at[0, pipe], own_sem.at[0])
    own_index = pltpu.make_async_copy(sendi_v.at[0], index_out.at[0, pipe], own_sem.at[1])
    own_rows.start()
    own_index.start()

    def arrive(k, carry):
        d = partner(me, k, n)
        for copy in (row_copy(k, other, d), index_copy(k, other, d)):
            copy.wait_send()

        @pl.when(k > 0)
        def _():
            for copy in (row_copy(k, pipe, d), index_copy(k, pipe, d)):
                copy.wait_send()

        for s_is_other in (True, False):
            s = other if s_is_other else pipe

            def wait_from():
                pltpu.make_async_remote_copy(
                    src_ref=send_v.at[k, pipe], dst_ref=rows_out.at[k, s],
                    send_sem=send_sem.at[k, pipe], recv_sem=recv_sem.at[k, s],
                    device_id={"dp": d, "pipe": other}, device_id_type=pl.DeviceIdType.MESH,
                ).wait_recv()
                pltpu.make_async_remote_copy(
                    src_ref=sendi_v.at[k], dst_ref=index_out.at[k, s],
                    send_sem=isend_sem.at[k, pipe], recv_sem=irecv_sem.at[k, s],
                    device_id={"dp": d, "pipe": other}, device_id_type=pl.DeviceIdType.MESH,
                ).wait_recv()

            if s_is_other:
                wait_from()
            else:
                pl.when(k > 0)(wait_from)
        return carry

    lax.fori_loop(0, n, arrive, 0)
    own_rows.wait()
    own_index.wait()


def exchange(ids, embedded, gain, proj_grad, weight, stream, n, n_mp, cap, block_rows):
    tokens, width = embedded.shape
    inner = proj_grad.shape[1]
    half = width // 2
    chunk = min(256, width)
    any_space = pl.BlockSpec(memory_space=pl.ANY)
    vmem = pl.BlockSpec(memory_space=pltpu.VMEM)
    dma = pltpu.SemaphoreType.DMA
    return pl.pallas_call(
        functools.partial(
            exchange_kernel, n, n_mp, cap, block_rows, width * n_mp, chunk, tokens
        ),
        out_shape=(
            jax.ShapeDtypeStruct((n, 2, cap, half), jnp.bfloat16),
            jax.ShapeDtypeStruct((n, 2, 1, cap), jnp.int32),
        ),
        in_specs=[vmem, vmem] + [any_space] * 4,
        out_specs=(any_space, any_space),
        scratch_shapes=[
            pltpu.VMEM((tokens, width), jnp.bfloat16),
            pltpu.VMEM((tokens, inner), jnp.bfloat16),
            pltpu.VMEM((width, inner), jnp.bfloat16),
            pltpu.VMEM((tokens, width), jnp.bfloat16),
            pltpu.VMEM((tokens, width), jnp.float32),
            pltpu.VMEM((tokens, width), jnp.bfloat16),
            pltpu.VMEM((n, 2, cap, half), jnp.bfloat16),
            pltpu.VMEM((n, 1, cap), jnp.int32),
            pltpu.VMEM((8, tokens), jnp.float32),
            pltpu.VMEM((8, tokens), jnp.float32),
            pltpu.VMEM((1, tokens), jnp.int32),
            pltpu.VMEM((8, tokens), jnp.bfloat16),
            dma((3,)),
            dma((width // chunk,)),
            dma,
            dma,
            dma((n, 2)),
            dma((n, 2)),
            dma((n, 2)),
            dma((n, 2)),
            dma((2,)),
        ],
        compiler_params=pltpu.CompilerParams(
            collective_id=0, has_side_effects=True, vmem_limit_bytes=VMEM_LIMIT
        ),
    )(ids, gain, embedded, proj_grad, weight, stream)


def table_kernel(cap, index_ref, rows_ref, out_ref, wide_v):
    lines = wide_v.shape[0] // cap
    blocks = rows_ref.shape[0]
    pieces = 16
    while out_ref.shape[0] % (8 * pieces):
        pieces //= 2
    zero_rows = out_ref.shape[0] // pieces

    def clear(i, carry):
        out_ref[pl.ds(pl.multiple_of(i * zero_rows, 8), zero_rows), :] = jnp.zeros(
            (zero_rows, LANES), jnp.float32
        )
        return carry

    lax.fori_loop(0, pieces, clear, 0)

    def block(b, carry):
        for j in range(lines):
            wide_v[pl.ds(j, cap, stride=lines), :] = rows_ref[b, :, j * LANES:(j + 1) * LANES].astype(
                jnp.float32
            )

        def add(g, carry):
            for u in range(8):
                c = g * 8 + u
                v = pl.multiple_of(index_ref[b, 0, c] * lines, lines)
                out_ref[pl.ds(v, lines), :] += wide_v[pl.ds(pl.multiple_of(c * lines, lines), lines), :]
            return carry

        return lax.fori_loop(0, cap // 8, add, carry)

    lax.fori_loop(0, blocks, block, 0)


def table(index, rows, block_rows):
    n, stacks, cap, half = rows.shape
    lines = half // LANES
    return pl.pallas_call(
        functools.partial(table_kernel, cap),
        out_shape=jax.ShapeDtypeStruct((block_rows * lines, LANES), jnp.float32),
        in_specs=[
            pl.BlockSpec(memory_space=pltpu.SMEM),
            pl.BlockSpec(memory_space=pltpu.VMEM),
        ],
        out_specs=pl.BlockSpec(memory_space=pltpu.VMEM),
        scratch_shapes=[pltpu.VMEM((cap * lines, LANES), jnp.float32)],
        compiler_params=pltpu.CompilerParams(vmem_limit_bytes=VMEM_LIMIT),
    )(index.reshape(n * stacks, 1, cap), rows.reshape(n * stacks, cap, half))


def on_device(token_ids, embedded, norm_gain, proj_grad, proj_weight, stream_grad):
    n = lax.axis_size("dp")
    tokens = token_ids.shape[1]
    cap = max(2, 2 * tokens // n)
    block_rows = VOCAB // n
    rows, index = exchange(
        token_ids, embedded[0], norm_gain, proj_grad[0], proj_weight[0], stream_grad[0],
        n, lax.axis_size("mp"), cap, block_rows,
    )
    half = rows.shape[-1]
    return table(index, rows, block_rows).reshape(block_rows, 1, half)


def solution(mesh):
    return jax.shard_map(
        on_device,
        mesh=mesh,
        in_specs=(
            P("pipe", "dp"),
            P("pipe", "dp", "mp"),
            P("pipe", "mp"),
            P("pipe", "dp", None),
            P("pipe", "mp", None),
            P("pipe", "dp", "mp"),
        ),
        out_specs=P("dp", "mp", "pipe"),
        check_vma=False,
    )
```

time: 246 us -> 139 us (0.57)
  the two profiles are of different devices: /device:TPU:0 before, /device:TPU:8 now
where the time goes in v1:
time: 139 us; the launch traced here: 137 us
  Pallas kernels  137 us (99%)
    pallas_call x1, Pallas kernels, exchange(): pl.pallas_call(functools.partial(exchange_kernel, n, n_mp, cap, block_row...  116 us
    pallas_call x1, Pallas kernels, table(): pl.pallas_call(functools.partial(table_kernel, cap), out_shape=jax.ShapeD...  21.3 us

profile of v1, /device:TPU:8, one launch (start us, length us, event | category | flops | bytes accessed | tf_op | source)
XLA Modules:
  0.0 137.1 jit_solution(9333554399480464007)
XLA Ops:
  0.0 115.8 %shard_map.64 = (bf16[8,2,128,1024]{3,2,1,0:T(8,128)(2,1)}, s32[8,2,1,128]{3,2,1,0:T(1,128)}) custom-call(s32[1,512]{1,0:T(1,128)} %ids_ref.1, f32[1,2048]{1,0:T(1,128)} %gain_ref.1, bf16[512,2048]{1,0:T(8,128)(2,1)} %bitcast.9, bf16[512,2048]{1,0:T(8,128)(2,1)} %bitcast.10, bf16[2048,2048]{1,0:T(8,128)(2,1)} %bitcast.7, bf16[512,2048]{1,0:T(8,128)(2,1)} %bitcast.11), custom_call_target="tpu_custom_call" | custom-call | tf_op jit(solution)/shard_map/pallas_call | solution.py:241
  115.8 21.3 %shard_map.65 = f32[32128,128]{1,0:T(8,128)} custom-call(s32[16,1,128]{2,1,0:T(1,128)} %bitcast.12, bf16[16,128,1024]{2,1,0:T(8,128)(2,1)} %bitcast.8), custom_call_target="tpu_custom_call" | custom-call | tf_op jit(solution)/shard_map/pallas_call | solution.py:317
